TPU v7x, 512 devices: a whole 4x8x8 slice. The times are simulated.
512 devices in a mesh: row: 64 (over x, y, core), col: 8 (over z).
Axes of the slice: x: 4, y: 8, z: 8, core: 2. Of those that a mesh axis runs over, the one named last changes fastest.
Arguments:
- matrix: float32 [16384, 4096], P('row', 'col'), may hold values from -7.8125 to 7.8125
Outputs:
- r_top: float32 [512, 4096], P(None, 'col')
- basis: float32 [16384, 512], P('row')
All inputs are finite; a program needn't handle non-finite values.
Results may differ from a plain program's by a relative error of at most 0.0003.
Values sent between devices are 32-bit elements; how exact they have to be, the bound alone decides.
No kernel may reach another device: no remote copies, remote signals or barrier semaphores. Data moves between devices by JAX's collectives and lax.ppermute only.
A program may use at most 64 MiB of HBM per device.

v0:
```python
import math

import jax
import jax.numpy as jnp
from jax import lax
from jax.sharding import Mesh
from jax.sharding import PartitionSpec as P

PANEL = 256
ROW = ("row_0", "row_1", "row_2")


def from_root(array, axis, root):
    return lax.dynamic_index_in_dim(lax.all_gather(array, axis), root, 0, keepdims=False)


def filled_up(lines, devices):
    spare = -len(lines) % devices
    return jnp.pad(lines, [(0, spare)] + [(0, 0)] * (lines.ndim - 1))


def copy_for_each(array, axis):
    devices = lax.axis_size(axis)
    return lax.all_to_all(
        jnp.broadcast_to(array[None], (devices, *array.shape)), axis, 0, 0, tiled=True
    )


def joined_along(blocks, dim):
    blocks = jnp.moveaxis(blocks, 0, dim)
    shape = blocks.shape
    return blocks.reshape(*shape[:dim], shape[dim] * shape[dim + 1], *shape[dim + 2 :])


def gathered_copies(array, axis, dim):
    blocks = copy_for_each(array, axis)
    return joined_along(blocks, dim)


def cut_along(array, dim, devices):
    shape = array.shape
    blocks = array.reshape(*shape[:dim], devices, shape[dim] // devices, *shape[dim + 1 :])
    return jnp.moveaxis(blocks, dim, 0)


def sent_and_summed(array, axis, dim):
    blocks = cut_along(array, dim, lax.axis_size(axis))
    arrived = lax.all_to_all(blocks, axis, split_axis=0, concat_axis=0, tiled=True)
    return arrived.sum(axis=0)


def sum_by_parts(array, axes):
    lines = array.reshape(-1, array.shape[-1])
    padded = filled_up(lines, lax.axis_size(axes))
    whole = gathered_copies(sent_and_summed(padded, axes, 0), axes, 0)
    return lax.slice_in_dim(whole, 0, len(lines)).reshape(array.shape)


def gather_axes(array, axes, dim):
    far, near = axes
    first = copy_for_each(array, far)
    blocks = jnp.swapaxes(copy_for_each(first, near), 0, 1)
    return joined_along(blocks.reshape(-1, *array.shape), dim)


def sum_in_two_steps(array, axes, dim):
    far, near = axes
    own = sent_and_summed(cut_along(array, dim, lax.axis_size(far)), near, dim + 1)
    return jnp.sum(lax.all_to_all(own, far, 0, 0, tiled=True), axis=0)


def nested_sum(array, axes):
    padded = filled_up(array, lax.axis_size(axes[0]) * lax.axis_size(axes[1]))
    whole = gather_axes(sum_in_two_steps(padded, axes, 0), axes, 0)
    return lax.slice_in_dim(whole, 0, len(array)).reshape(array.shape)


def in_one(arrays, axis):
    ends = [0]
    for a in arrays:
        ends.append(ends[-1] + a.size)
    so_far = nested_sum(jnp.concatenate([a.ravel() for a in arrays]), axis)
    return tuple((so_far[b:e].reshape(a.shape) for a, b, e in zip(arrays, ends, ends[1:])))


def inner(left, right):
    return lax.dot_general(
        left,
        right,
        (((0,), (0,)), ((), ())),
        precision=lax.Precision.HIGHEST,
        preferred_element_type=jnp.float32,
    )


def product(left, right):
    return jnp.dot(left, right, precision=lax.Precision.HIGHEST, preferred_element_type=jnp.float32)


def factor(gram, valid):
    width = gram.shape[0]
    identity = jnp.eye(width, dtype=jnp.float32)
    safe_gram = jnp.where(valid, gram, identity)
    lower_factor = jnp.linalg.cholesky(safe_gram)
    lower_inverse = lax.linalg.triangular_solve(lower_factor, identity, left_side=True, lower=True)
    return (lower_factor.T, lower_inverse.T)


def body(matrix):
    panel_cols = PANEL
    local_width = matrix.shape[1]
    rows_all = matrix.shape[0] * lax.axis_size(ROW)
    holder = lax.axis_index("col") == 0
    everywhere = jnp.array(True)
    panels = from_root(matrix, "col", 0)
    first_panel = panels[:, :panel_cols]
    second_panel = panels[:, panel_cols:]
    first_gram = sum_by_parts(inner(first_panel, first_panel), ROW)
    upper_first, inverse_first = factor(first_gram, everywhere)
    basis_first = product(first_panel, inverse_first)
    local_terms = inner(basis_first, matrix)
    local_terms = jnp.concatenate([local_terms, inner(basis_first, second_panel)], axis=1)
    summed, panel_gram = in_one(
        (local_terms, inner(second_panel, second_panel)), (("row_0", "row_1"), "row_2")
    )
    projected = summed[:, :local_width]
    coupling = summed[:, local_width:]
    remainder = matrix - product(basis_first, projected)
    second_updated = second_panel - product(basis_first, coupling)
    second_gram = panel_gram - inner(coupling, coupling)
    upper_second, inverse_second = factor(second_gram, everywhere)
    basis_second = product(second_updated, inverse_second)
    second_proj = sum_by_parts(inner(basis_second, remainder), ROW)
    zeros = jnp.zeros((panel_cols, panel_cols), jnp.float32)
    first_rows = jnp.where(
        holder, jnp.concatenate([upper_first, projected[:, panel_cols:]], axis=1), projected
    )
    second_rows = jnp.where(
        holder,
        jnp.concatenate([zeros, upper_second, second_proj[:, 2 * panel_cols :]], axis=1),
        second_proj,
    )
    top = jnp.concatenate([first_rows, second_rows], axis=0)
    basis = jnp.concatenate([basis_first, basis_second], axis=1) * math.sqrt(rows_all)
    return (top, basis)


def solution(mesh):
    finer = Mesh(
        mesh.devices.reshape(4, 8, 2, mesh.shape["col"]), ("row_0", "row_1", "row_2", "col")
    )
    placed = (P(ROW, "col"),)
    return jax.shard_map(
        body, mesh=finer, in_specs=placed, out_specs=(P(None, "col"), P(ROW, None)), check_vma=False
    )
```

profile of v0, /device:TPU:1, one launch (start us, length us, event | category | flops | bytes accessed | tf_op | source)
XLA Modules:
  0.0 364.5 jit_solution(10112431236812248028)
XLA Ops:
  7.2 0.7 all-gather.3.cloned.1.call-update
  7.9 65.7 %all-gather.3.cloned.1.call-done = f32[2048,512]{1,0:T(8,128)} async-done(((f32[256,512]{1,0:T(8,128)}), f32[2048,512]{1,0:T(8,128)}) %all-gather.3.cloned.1.call-update) | async-done | bytes 4194320 | tf_op jit(solution)/shard_map/all_gather | solution.py:14
  73.6 1.6 fusion.16
  75.2 0.8 reshape.61
  76.0 10.5 %all-to-all-start = ((f32[64,4,256]{2,1,0:T(4,128)}), f32[64,4,256]{2,1,0:T(4,128)S(1)}, u32[]{:S(2)}, u32[]{:S(2)}) async-start(f32[64,4,256]{2,1,0:T(4,128)} %reshape.61), calls=%async_computation | async-start | bytes 524288 | tf_op jit(solution)/shard_map/all_to_all | solution.py:48
  86.5 12.0 %all-to-all-done = f32[64,4,256]{2,1,0:T(4,128)S(1)} async-done(((f32[64,4,256]{2,1,0:T(4,128)}), f32[64,4,256]{2,1,0:T(4,128)S(1)}, u32[]{:S(2)}, u32[]{:S(2)}) %all-to-all-start) | async-done | bytes 262176 | tf_op jit(solution)/shard_map/all_to_all | solution.py:48
  98.6 0.7 broadcast_in_dim.11
  99.3 6.5 %all-to-all-start.1 = ((f32[64,4,256]{2,1,0:T(4,128)}), f32[64,4,256]{2,1,0:T(4,128)S(1)}, u32[]{:S(2)}, u32[]{:S(2)}) async-start(f32[64,4,256]{2,1,0:T(4,128)} %broadcast_in_dim.11), calls=%async_computation.1 | async-start | bytes 524288 | tf_op jit(solution)/shard_map/all_to_all | solution.py:24
  105.8 1.6 convolution_bitcast_fusion
  107.6 10.0 %all-to-all-done.1 = f32[64,4,256]{2,1,0:T(4,128)S(1)} async-done(((f32[64,4,256]{2,1,0:T(4,128)}), f32[64,4,256]{2,1,0:T(4,128)S(1)}, u32[]{:S(2)}, u32[]{:S(2)}) %all-to-all-start.1) | async-done | bytes 262176 | tf_op jit(solution)/shard_map/all_to_all | solution.py:24
  117.9 11.7 %cholesky.130 = f32[128,128]{1,0:T(8,128)S(1)} custom-call(f32[128,128]{1,0:T(8,128)S(1)} %cholesky.194), custom_call_target="Cholesky" | custom-call | tf_op jit(solution)/shard_map/jit(cholesky)/cholesky | solution.py:104
  129.7 9.8 %custom-call.13 = f32[1,128,128]{1,2,0:T(8,128)S(1)} custom-call(f32[1,128,128]{2,1,0:T(8,128)S(1)} %get-tuple-element.59), custom_call_target="InvertDiagBlocksLowerTriangular" | custom-call | tf_op jit(solution)/shard_map/jit(cholesky)/cholesky | solution.py:104
  140.0 11.7 %cholesky.147 = f32[128,128]{1,0:T(8,128)S(1)} custom-call(f32[128,128]{1,0:T(8,128)S(1)} %convolution_subtract_fusion.6), custom_call_target="Cholesky" | custom-call | tf_op jit(solution)/shard_map/jit(cholesky)/cholesky | solution.py:104
  151.8 0.7 compare_reduce_fusion.2
  153.7 0.7 fusion.21
  154.5 3.9 %while.4 = (s32[]{:T(128)}, f32[256,256]{1,0:T(8,128)S(1)}, s32[2,2]{1,0:T(2,128)S(1)}, f32[2,128,128]{2,1,0:T(8,128)S(1)}, s32[]{:T(128)}) while((s32[]{:T(128)}, f32[256,256]{1,0:T(8,128)S(1)}, s32[2,2]{1,0:T(2,128)S(1)}, f32[2,128,128]{2,1,0:T(8,128)S(1)}, s32[]{:T(128)}) %tuple.52), condition=%wide.while_cond, body=%wide.while_body.sunk | while | flops 2 | bytes 131189 | solution.py:105
  155.1 1.3 bitcast_dynamic-update-slice_fusion.4
  157.0 1.3 bitcast_dynamic-update-slice_fusion.4
  158.3 19.9 %custom-call.14 = f32[2,128,128]{1,2,0:T(8,128)S(1)} custom-call(f32[2,128,128]{2,1,0:T(8,128)S(1)} %get-tuple-element.18), custom_call_target="InvertDiagBlocksLowerTriangular" | custom-call | tf_op jit(solution)/shard_map/triangular_solve/custom-call.0 | solution.py:105
  179.1 1.4 fusion
  180.5 0.6 fusion.42
  181.1 1.3 fusion.19
  183.2 0.6 copy.36
  183.9 4.7 %all_to_all.45 = f32[2,32,4096]{2,1,0:T(8,128)S(1)} all-to-all(f32[2,32,4096]{2,1,0:T(8,128)S(1)} %copy.36), channel_id=1, replica_groups=mesh['row_0'=4,'row_1'=8,'row_2'=2,'col'=8] {'row_2'}, dimensions={0} | all-to-all | bytes 2097152 | tf_op jit(solution)/shard_map/all_to_all | solution.py:48
  189.2 19.1 %all_to_all.47 = f32[32,1,4096]{2,1,0:T(1,128)S(1)} all-to-all(f32[32,1,4096]{2,1,0:T(1,128)S(1)} %all_to_all.31), channel_id=1, replica_groups=mesh['row_0'=4,'row_1'=8,'row_2'=2,'col'=8] {'row_0','row_1'}, dimensions={0} | all-to-all | bytes 1048576 | tf_op jit(solution)/shard_map/all_to_all | solution.py:69
  208.7 1.3 broadcast_in_dim.12
  209.9 8.1 %all-to-all-start.4 = ((f32[32,1,4096]{2,1,0:T(1,128)}), f32[32,1,4096]{2,1,0:T(1,128)S(1)}, u32[]{:S(2)}, u32[]{:S(2)}) async-start(f32[32,1,4096]{2,1,0:T(1,128)} %broadcast_in_dim.12), calls=%async_computation.4 | async-start | bytes 1048576 | tf_op jit(solution)/shard_map/all_to_all | solution.py:24
  218.0 14.6 %all-to-all-done.4 = f32[32,1,4096]{2,1,0:T(1,128)S(1)} async-done(((f32[32,1,4096]{2,1,0:T(1,128)}), f32[32,1,4096]{2,1,0:T(1,128)S(1)}, u32[]{:S(2)}, u32[]{:S(2)}) %all-to-all-start.4) | async-done | bytes 524320 | tf_op jit(solution)/shard_map/all_to_all | solution.py:24
  233.0 7.3 %all_to_all.46 = f32[2,32,4096]{2,1,0:T(8,128)S(1)} all-to-all(f32[2,32,4096]{2,1,0:T(8,128)S(1)} %broadcast_in_dim.14), channel_id=1, replica_groups=mesh['row_0'=4,'row_1'=8,'row_2'=2,'col'=8] {'row_2'}, dimensions={0} | all-to-all | bytes 2097152 | tf_op jit(solution)/shard_map/all_to_all | solution.py:24
  241.0 0.6 reshape.65
  243.0 11.7 %cholesky.164 = f32[128,128]{1,0:T(8,128)S(1)} custom-call(f32[128,128]{1,0:T(8,128)S(1)} %cholesky.197), custom_call_target="Cholesky" | custom-call | tf_op jit(solution)/shard_map/jit(cholesky)/cholesky | solution.py:104
  254.8 9.8 %custom-call.15 = f32[1,128,128]{1,2,0:T(8,128)S(1)} custom-call(f32[1,128,128]{2,1,0:T(8,128)S(1)} %get-tuple-element.55), custom_call_target="InvertDiagBlocksLowerTriangular" | custom-call | tf_op jit(solution)/shard_map/jit(cholesky)/cholesky | solution.py:104
  265.3 0.6 convolution_subtract_fusion
  265.9 0.6 compare_reduce_fusion.1
  266.6 11.9 %cholesky.181 = f32[128,128]{1,0:T(8,128)S(1)} custom-call(f32[128,128]{1,0:T(8,128)S(1)} %convolution_subtract_fusion.5), custom_call_target="Cholesky" | custom-call | tf_op jit(solution)/shard_map/jit(cholesky)/cholesky | solution.py:104
  278.5 0.6 compare_reduce_fusion
  280.4 3.9 %while.5 = (s32[]{:T(128)}, f32[256,256]{1,0:T(8,128)S(1)}, s32[2,2]{1,0:T(2,128)S(1)}, f32[2,128,128]{2,1,0:T(8,128)S(1)}, s32[]{:T(128)}) while((s32[]{:T(128)}, f32[256,256]{1,0:T(8,128)S(1)}, s32[2,2]{1,0:T(2,128)S(1)}, f32[2,128,128]{2,1,0:T(8,128)S(1)}, s32[]{:T(128)}) %tuple.60), condition=%wide.while_cond.clone, body=%wide.while_body.clone.sunk | while | flops 2 | bytes 131189 | solution.py:105
  281.1 1.3 bitcast_dynamic-update-slice_fusion.5
  283.0 1.3 bitcast_dynamic-update-slice_fusion.5
  284.3 19.7 %custom-call.16 = f32[2,128,128]{1,2,0:T(8,128)S(1)} custom-call(f32[2,128,128]{2,1,0:T(8,128)S(1)} %get-tuple-element.19), custom_call_target="InvertDiagBlocksLowerTriangular" | custom-call | tf_op jit(solution)/shard_map/triangular_solve/custom-call.0 | solution.py:105
  304.9 1.5 convolution_subtract_fusion.1
  306.9 0.6 fusion.43
  307.6 23.4 %all_to_all.48 = f32[64,4,512]{2,1,0:T(4,128)S(1)} all-to-all(f32[64,4,512]{2,1,0:T(4,128)S(1)} %reshape.67), channel_id=1, replica_groups=mesh['row_0'=4,'row_1'=8,'row_2'=2,'col'=8] {'row_0','row_1','row_2'}, dimensions={0} | all-to-all | bytes 1048576 | tf_op jit(solution)/shard_map/all_to_all | solution.py:48
  331.1 0.9 broadcast_in_dim.15
  332.0 6.3 %all-to-all-start.7 = ((f32[64,4,512]{2,1,0:T(4,128)}), f32[64,4,512]{2,1,0:T(4,128)S(1)}, u32[]{:S(2)}, u32[]{:S(2)}) async-start(f32[64,4,512]{2,1,0:T(4,128)} %broadcast_in_dim.15), calls=%async_computation.7 | async-start | bytes 1048576 | tf_op jit(solution)/shard_map/all_to_all | solution.py:24
  338.6 1.0 copy.47
  339.9 15.7 %all-to-all-done.7 = f32[64,4,512]{2,1,0:T(4,128)S(1)} async-done(((f32[64,4,512]{2,1,0:T(4,128)}), f32[64,4,512]{2,1,0:T(4,128)S(1)}, u32[]{:S(2)}, u32[]{:S(2)}) %all-to-all-start.7) | async-done | bytes 524320 | tf_op jit(solution)/shard_map/all_to_all | solution.py:24
  356.2 1.3 copy.46
  (75 shorter events, 12.0 us)
Async XLA Ops:
  7.2 66.4 %all-gather.3.cloned.1.call-start = ((), (), s32[]{:S(2)}) async-start(), calls=%async_computation.8 | async-start | bytes 4718592 | tf_op jit(solution)/shard_map/all_gather | solution.py:14
  76.0 22.5 %all-to-all-start = ((f32[64,4,256]{2,1,0:T(4,128)}), f32[64,4,256]{2,1,0:T(4,128)S(1)}, u32[]{:S(2)}, u32[]{:S(2)}) async-start(f32[64,4,256]{2,1,0:T(4,128)} %reshape.61), calls=%async_computation | async-start | bytes 524288 | tf_op jit(solution)/shard_map/all_to_all | solution.py:48
  99.3 81.2 %copy-start = (f32[256,512]{1,0:T(8,128)S(1)}, f32[256,512]{1,0:T(8,128)}, u32[]{:S(2)}) copy-start(f32[256,512]{1,0:T(8,128)} %param.4) | copy-start | bytes 1572868
  99.3 18.3 %all-to-all-start.1 = ((f32[64,4,256]{2,1,0:T(4,128)}), f32[64,4,256]{2,1,0:T(4,128)S(1)}, u32[]{:S(2)}, u32[]{:S(2)}) async-start(f32[64,4,256]{2,1,0:T(4,128)} %broadcast_in_dim.11), calls=%async_computation.1 | async-start | bytes 524288 | tf_op jit(solution)/shard_map/all_to_all | solution.py:24
  209.9 22.6 %all-to-all-start.4 = ((f32[32,1,4096]{2,1,0:T(1,128)}), f32[32,1,4096]{2,1,0:T(1,128)S(1)}, u32[]{:S(2)}, u32[]{:S(2)}) async-start(f32[32,1,4096]{2,1,0:T(1,128)} %broadcast_in_dim.12), calls=%async_computation.4 | async-start | bytes 1048576 | tf_op jit(solution)/shard_map/all_to_all | solution.py:24
  331.0 8.8 %copy-start.1 = (f32[256,256]{0,1:T(8,128)S(1)}, f32[256,256]{0,1:T(8,128)}, u32[]{:S(2)}) copy-start(f32[256,256]{0,1:T(8,128)} %get-tuple-element.48) | copy-start | bytes 786436
  332.0 23.6 %all-to-all-start.7 = ((f32[64,4,512]{2,1,0:T(4,128)}), f32[64,4,512]{2,1,0:T(4,128)S(1)}, u32[]{:S(2)}, u32[]{:S(2)}) async-start(f32[64,4,512]{2,1,0:T(4,128)} %broadcast_in_dim.15), calls=%async_computation.7 | async-start | bytes 1048576 | tf_op jit(solution)/shard_map/all_to_all | solution.py:24
Sparse Core Ops, SparseCore 0:
  10.0 63.4 all-gather.2
where the time goes:
time: 368 us; the launch traced here: 365 us
  waiting for transfers between devices  119 us (32%)
  other arithmetic  110 us (30%)
  blocking collectives  54.5 us (15%)
  starting transfers between devices  31.4 us (9%)
  local copies, waits for them, and re-layouts  19.3 us (5%)
  between operations  17.3 us (5%)
  matrix products  13.1 us (4%)
    another operation x13, other arithmetic, factor(): lower_factor = jnp.linalg.cholesky(safe_gram)  68.7 us
    all_gather x1, waiting for transfers between devices, from_root(): lax.all_gather(array, axis)  65.7 us
    all_to_all x3, waiting for transfers between devices, copy_for_each(): lax.all_to_all(jnp.broadcast_to(array[None], (devices, *array.shape)), ax...  40.3 us
    another operation x3, other arithmetic, factor(): lax.linalg.triangular_solve(lower_factor, identity, left_side=True, lower...  39.6 us
    all_to_all x2, blocking collectives, sent_and_summed(): lax.all_to_all(blocks, axis, split_axis=0, concat_axis=0, tiled=True)  28.1 us
    all_to_all x3, starting transfers between devices, copy_for_each(): lax.all_to_all(jnp.broadcast_to(array[None], (devices, *array.shape)), ax...  20.8 us
    all_to_all x1, blocking collectives, sum_in_two_steps(): return jnp.sum(lax.all_to_all(own, far, 0, 0, tiled=True), axis=0)  19.1 us
    all_to_all x1, waiting for transfers between devices, sent_and_summed(): lax.all_to_all(blocks, axis, split_axis=0, concat_axis=0, tiled=True)  12 us
  transfers between devices with their start and end apart: 5, of which 5 were waited for; matrix products, arithmetic and copies ran while one was open for 1% of the time, Pallas kernels for 0%

commit v1 on v0

v1 whole, which is shorter than its diff:
```python
import math

import jax
import jax.numpy as jnp
from jax import lax
from jax.experimental import pallas as pl
from jax.experimental.pallas import tpu as pltpu
from jax.sharding import Mesh
from jax.sharding import PartitionSpec as P

PANEL = 256
WIDE = 2 * PANEL
TILE = 128
STEP = 32
ROW = ("x", "y", "core")
PLANE = ("x", "y")
HIGHEST = lax.Precision.HIGHEST


def inner(left, right):
    return lax.dot_general(
        left,
        right,
        (((0,), (0,)), ((), ())),
        precision=HIGHEST,
        preferred_element_type=jnp.float32,
    )


def product(left, right):
    return jnp.dot(left, right, precision=HIGHEST, preferred_element_type=jnp.float32)


PLACES = {0: (0, 0), 3: (0, 4), 1: (1, 0), 2: (1, 3)}


def packed_gram(panels):
    rows = {}
    for i in range(4):
        rows[i] = inner(panels[:, i * TILE : (i + 1) * TILE], panels[:, i * TILE :])
    return jnp.concatenate(
        [jnp.concatenate([rows[0], rows[3]], 1), jnp.concatenate([rows[1], rows[2]], 1)], 0
    )


def factor_kernel(packed_ref, out_ref):
    row8 = lax.broadcasted_iota(jnp.int32, (8, TILE), 0)
    lane = lax.broadcasted_iota(jnp.int32, (8, TILE), 1)
    tiles, groups = WIDE // TILE, STEP // 8
    for i, (r, c) in PLACES.items():
        out_ref[i * TILE : (i + 1) * TILE, i * TILE :] = packed_ref[
            r * TILE : (r + 1) * TILE, c * TILE : (c + 4 - i) * TILE
        ]

    def outer(t, _):
        base = pl.multiple_of(t * TILE, TILE)
        for u in range(TILE // STEP):
            first = pl.multiple_of(base + u * STEP, STEP)
            block = out_ref[pl.ds(first, STEP), pl.ds(base, TILE)]
            cols = []
            for q in range(STEP):
                spread = jnp.broadcast_to(block[:, u * STEP + q : u * STEP + q + 1], (STEP, TILE))
                cols.append([spread[8 * v : 8 * v + 8] for v in range(groups)])
            rows = []
            for v in range(groups):
                rows.append([])
                for w in range(tiles):
                    values = out_ref[pl.ds(first + 8 * v, 8), TILE * w : TILE * (w + 1)]
                    here = (lane >= u * STEP) & (lane < (u + 1) * STEP) & (t == w)
                    unit = jnp.where(lane - u * STEP == row8 + 8 * v, 1.0, 0.0)
                    rows[v].append(jnp.where(here, unit, values))
            pivots = [None] * groups
            for k in range(STEP):
                vk, sk = k // 8, k % 8
                pivot = jnp.broadcast_to(cols[k][vk][sk : sk + 1], (8, TILE))
                inverse = 1.0 / pivot
                pivots[vk] = pivot if sk == 0 else jnp.where(row8 == sk, pivot, pivots[vk])
                scaled = {}
                for v in range(vk, groups):
                    s = cols[k][v] * inverse
                    scaled[v] = jnp.where(row8 > sk, s, 0.0) if v == vk else s
                for j in range(k + 1, STEP):
                    other = jnp.broadcast_to(cols[k][j // 8][j % 8 : j % 8 + 1], (8, TILE))
                    for v in range(j // 8, groups):
                        cols[j][v] = cols[j][v] - scaled[v] * other
                for w in range(tiles):
                    other = jnp.broadcast_to(rows[vk][w][sk : sk + 1], (8, TILE))
                    for v in range(vk, groups):
                        rows[v][w] = rows[v][w] - scaled[v] * other
            for v in range(groups):
                scale = lax.rsqrt(pivots[v])
                for w in range(tiles):
                    out_ref[pl.ds(first + 8 * v, 8), TILE * w : TILE * (w + 1)] = rows[v][w] * scale
            if u < TILE // STEP - 1:
                rest = TILE - (u + 1) * STEP
                done = out_ref[pl.ds(first, STEP), :]
                left = out_ref[pl.ds(first, STEP), pl.ds(base, TILE)][:, (u + 1) * STEP :]
                old = out_ref[pl.ds(first + STEP, rest), :]
                col = lax.broadcasted_iota(jnp.int32, (rest, WIDE), 1)
                old = jnp.where((col >= first) & (col < first + STEP), 0.0, old)
                out_ref[pl.ds(first + STEP, rest), :] = old - inner(left, done)

        done = out_ref[pl.ds(base, TILE), :]
        row = lax.broadcasted_iota(jnp.int32, (TILE, WIDE), 0) + base
        col = lax.broadcasted_iota(jnp.int32, (TILE, WIDE), 1)
        done = jnp.where((col <= row) | (col >= base + TILE), done, 0.0)

        def below(i, _):
            start = pl.multiple_of(i * TILE, TILE)
            old = out_ref[pl.ds(start, TILE), :]
            old = jnp.where((col >= base) & (col < base + TILE), 0.0, old)
            out_ref[pl.ds(start, TILE), :] = old - inner(
                out_ref[pl.ds(base, TILE), pl.ds(start, TILE)], done
            )
            return 0

        lax.fori_loop(t + 1, tiles, below, 0)
        return 0

    lax.fori_loop(0, tiles, outer, 0)
    row = lax.broadcasted_iota(jnp.int32, (WIDE, WIDE), 0)
    col = lax.broadcasted_iota(jnp.int32, (WIDE, WIDE), 1)
    out_ref[...] = jnp.where(col <= row, out_ref[...], 0.0)


def inverse_factor(packed):
    vmem = pl.BlockSpec(memory_space=pltpu.VMEM)
    return pl.pallas_call(
        factor_kernel,
        out_shape=jax.ShapeDtypeStruct((WIDE, WIDE), jnp.float32),
        in_specs=[vmem],
        out_specs=vmem,
        compiler_params=pltpu.CompilerParams(vmem_limit_bytes=16 * 2**20),
        cost_estimate=pl.CostEstimate(
            flops=2_000_000_000, bytes_accessed=2**21, transcendentals=0
        ),
    )(packed)


def exchange(blocks, axis):
    return lax.all_to_all(blocks, axis, 0, 0, tiled=True)


def copies(array, axis):
    return exchange(jnp.broadcast_to(array[None], (lax.axis_size(axis), *array.shape)), axis)


def scattered_sum(array):
    width = array.shape[1]
    half = exchange(array.reshape(2, -1, width), "core").sum(axis=0)
    chips = lax.axis_size(PLANE)
    return exchange(half.reshape(chips, -1, width), PLANE).sum(axis=0)


def gathered(part):
    half = copies(part, PLANE).reshape(-1, part.shape[1])
    return copies(half, "core").reshape(-1, part.shape[1])


def body(matrix):
    rows_all = matrix.shape[0] * lax.axis_size(ROW)
    blocks = lax.axis_size("col")
    gram_part = scattered_sum(packed_gram(matrix))
    own = exchange(matrix.reshape(blocks, -1, WIDE), "col")[0]
    panels = copies(own, "col").reshape(-1, WIDE)
    gram_part = copies(gram_part, "col")[0]
    gram = gathered(gram_part)
    inner_products = gathered(scattered_sum(inner(panels, matrix)))
    inverse = inverse_factor(gram)
    top = product(inverse, inner_products)
    row = lax.broadcasted_iota(jnp.int32, (WIDE, WIDE), 0)
    column = lax.broadcasted_iota(jnp.int32, (WIDE, WIDE), 1)
    top = jnp.where((row > column) & (lax.axis_index("col") == 0), 0.0, top)
    basis = product(panels, inverse.T) * math.sqrt(rows_all)
    return (top, basis)


def solution(mesh):
    finer = Mesh(
        mesh.devices.reshape(4, 8, 2, mesh.shape["col"]), ("x", "y", "core", "col")
    )
    return jax.shard_map(
        body,
        mesh=finer,
        in_specs=(P(ROW, "col"),),
        out_specs=(P(None, "col"), P(ROW, None)),
        check_vma=False,
    )
```

time: 368 us -> 185 us (0.50)
  other arithmetic: 110 us -> 1.1 us
  waiting for transfers between devices: 119 us -> 57.6 us
  Pallas kernels: 0 us -> 17.5 us
  between operations: 17.3 us -> 0.79 us
  starting transfers between devices: 31.4 us -> 47.7 us
  local copies, waits for them, and re-layouts: 19.3 us -> 5.52 us
  blocking collectives: 54.5 us -> 42 us
    another operation x16 -> x0, other arithmetic: 108 us -> none  [the longest x13 68.7 us: factor(): lower_factor = jnp.linalg.cholesky(safe_gram)]
    all_gather x1 -> x0, waiting for transfers between devices: 65.7 us -> none  [from_root(): lax.all_gather(array, axis)]
    pallas_call x0 -> x1, Pallas kernels: none -> 17.5 us  [inverse_factor(): pl.pallas_call(factor_kernel, out_shape=jax.ShapeDtypeStruct((WIDE, WIDE)...]
    all_to_all x4 -> x7, starting transfers between devices: 31.4 us -> 47.7 us  [exchange(): return lax.all_to_all(blocks, axis, 0, 0, tiled=True)]
    all_to_all x4, blocking collectives: 54.5 us -> 42 us  [exchange(): return lax.all_to_all(blocks, axis, 0, 0, tiled=True)]
    another operation x22 -> x0, local copies, waits for them, and re-layouts: 8.41 us -> none  [the longest x15 7.7 us: factor(): lax.linalg.triangular_solve(lower_factor, identity, left_side=True, lower...]
    all_to_all x4 -> x7, waiting for transfers between devices: 52.3 us -> 57.6 us  [exchange(): return lax.all_to_all(blocks, axis, 0, 0, tiled=True)]
    dot_general x10 -> x7, matrix products: 10.3 us -> 11.8 us  [the longest x5 7.95 us: inner(): lax.dot_general(left, right, (((0,), (0,)), ((), ())), precision=HIGHEST,...]
  transfers between devices with their start and end apart: 5 -> 7, of which waited for: 5 -> 6; matrix products, arithmetic and copies ran while one was open for 1% -> 2% of each run, Pallas kernels for 0% -> 10%
where the time goes in v1:
time: 185 us; the launch traced here: 184 us
  waiting for transfers between devices  57.6 us (31%)
  starting transfers between devices  47.7 us (26%)
  blocking collectives  42 us (23%)
  Pallas kernels  17.5 us (9%)
  matrix products  11.8 us (6%)
  local copies, waits for them, and re-layouts  5.52 us (3%)
    all_to_all x7, waiting for transfers between devices, exchange(): return lax.all_to_all(blocks, axis, 0, 0, tiled=True)  57.6 us
    all_to_all x7, starting transfers between devices, exchange(): return lax.all_to_all(blocks, axis, 0, 0, tiled=True)  47.7 us
    all_to_all x4, blocking collectives, exchange(): return lax.all_to_all(blocks, axis, 0, 0, tiled=True)  42 us
    pallas_call x1, Pallas kernels, inverse_factor(): pl.pallas_call(factor_kernel, out_shape=jax.ShapeDtypeStruct((WIDE, WIDE)...  17.5 us
    dot_general x5, matrix products, inner(): lax.dot_general(left, right, (((0,), (0,)), ((), ())), precision=HIGHEST,...  7.95 us
    broadcast_in_dim x9, local copies, waits for them, and re-layouts, copies(): jnp.broadcast_to(array[None], (lax.axis_size(axis), *array.shape))  4.23 us
    dot_general x2, matrix products, product(): jnp.dot(left, right, precision=HIGHEST, preferred_element_type=jnp.float32)  3.84 us
  transfers between devices with their start and end apart: 7, of which 6 were waited for; matrix products, arithmetic and copies ran while one was open for 2% of the time, Pallas kernels for 10%

profile of v1, /device:TPU:1, one launch (start us, length us, event | category | flops | bytes accessed | tf_op | source)
XLA Modules:
  0.0 184.0 jit_solution(4599394513530660739)
XLA Ops:
  0.6 1.6 fusion.12
  2.2 1.5 fusion.4
  3.7 1.4 fusion.6
  5.2 1.4 fusion.10
  6.6 10.7 %all_to_all.55 = f32[2,128,640]{2,1,0:T(8,128)S(1)} all-to-all(f32[2,128,640]{2,1,0:T(8,128)S(1)} %bitcast.29), channel_id=1, replica_groups=mesh['x'=4,'y'=8,'core'=2,'col'=8] {'core'}, dimensions={0} | all-to-all | bytes 1310720 | tf_op jit(solution)/shard_map/all_to_all | solution.py:141
  17.4 0.1 reshape.32
  17.5 14.6 %all_to_all.56 = f32[32,4,640]{2,1,0:T(4,128)S(1)} all-to-all(f32[32,4,640]{2,1,0:T(4,128)S(1)} %reshape.32), channel_id=1, replica_groups=mesh['x'=4,'y'=8,'core'=2,'col'=8] {'x','y'}, dimensions={0} | all-to-all | bytes 655360 | tf_op jit(solution)/shard_map/all_to_all | solution.py:141
  32.1 10.0 %all-to-all-start.5 = ((f32[8,32,512]{2,1,0:T(8,128)}), f32[8,32,512]{2,1,0:T(8,128)S(1)}, u32[]{:S(2)}, u32[]{:S(2)}) async-start(f32[8,32,512]{2,1,0:T(8,128)} %bitcast.3), calls=%async_computation.5 | async-start | bytes 1048576 | tf_op jit(solution)/shard_map/all_to_all | solution.py:141
  42.1 0.1 reduce_sum.37
  42.2 13.0 %all-to-all-done.5 = f32[8,32,512]{2,1,0:T(8,128)S(1)} async-done(((f32[8,32,512]{2,1,0:T(8,128)}), f32[8,32,512]{2,1,0:T(8,128)S(1)}, u32[]{:S(2)}, u32[]{:S(2)}) %all-to-all-start.5) | async-done | bytes 524320 | tf_op jit(solution)/shard_map/all_to_all | solution.py:141
  55.2 0.6 broadcast_in_dim.45
  55.8 3.4 %all-to-all-start.2 = ((f32[8,4,640]{2,1,0:T(4,128)}), f32[8,4,640]{2,1,0:T(4,128)S(1)}, u32[]{:S(2)}, u32[]{:S(2)}) async-start(f32[8,4,640]{2,1,0:T(4,128)} %broadcast_in_dim.45), calls=%async_computation.2 | async-start | bytes 163840 | tf_op jit(solution)/shard_map/all_to_all | solution.py:141
  59.2 7.3 %all-to-all-done.2 = f32[8,4,640]{2,1,0:T(4,128)S(1)} async-done(((f32[8,4,640]{2,1,0:T(4,128)}), f32[8,4,640]{2,1,0:T(4,128)S(1)}, u32[]{:S(2)}, u32[]{:S(2)}) %all-to-all-start.2) | async-done | bytes 81952 | tf_op jit(solution)/shard_map/all_to_all | solution.py:141
  66.5 0.9 broadcast_in_dim.51
  67.4 3.5 %all-to-all-start.6 = ((f32[8,32,512]{2,1,0:T(8,128)}), f32[8,32,512]{2,1,0:T(8,128)S(1)}, u32[]{:S(2)}, u32[]{:S(2)}) async-start(f32[8,32,512]{2,1,0:T(8,128)} %broadcast_in_dim.51), calls=%async_computation.6 | async-start | bytes 1048576 | tf_op jit(solution)/shard_map/all_to_all | solution.py:141
  70.9 12.1 %all-to-all-done.6 = f32[8,32,512]{2,1,0:T(8,128)S(1)} async-done(((f32[8,32,512]{2,1,0:T(8,128)}), f32[8,32,512]{2,1,0:T(8,128)S(1)}, u32[]{:S(2)}, u32[]{:S(2)}) %all-to-all-start.6) | async-done | bytes 524320 | tf_op jit(solution)/shard_map/all_to_all | solution.py:141
  83.0 0.2 copy.14
  83.2 2.1 %fusion.2 = f32[2,256,512]{2,1,0:T(8,128)S(1)} fusion(f32[2,256,256]{2,1,0:T(8,128)S(1)} %bitcast.31, f32[256,512]{1,0:T(8,128)} %param.1), kind=kOutput, calls=%fused_computation.6 | convolution fusion | flops 805306368 | bytes 2097152 | tf_op jit(solution)/shard_map/dot_general | solution.py:21
  85.3 11.8 %all_to_all.57 = f32[2,256,512]{2,1,0:T(8,128)S(1)} all-to-all(f32[2,256,512]{2,1,0:T(8,128)S(1)} %fusion.2), channel_id=1, replica_groups=mesh['x'=4,'y'=8,'core'=2,'col'=8] {'core'}, dimensions={0} | all-to-all | bytes 2097152 | tf_op jit(solution)/shard_map/all_to_all | solution.py:141
  97.1 0.8 broadcast_in_dim.47
  97.8 10.9 %all-to-all-start.3 = ((f32[32,4,640]{2,1,0:T(4,128)}), f32[32,4,640]{2,1,0:T(4,128)S(1)}, u32[]{:S(2)}, u32[]{:S(2)}) async-start(f32[32,4,640]{2,1,0:T(4,128)} %broadcast_in_dim.47), calls=%async_computation.3 | async-start | bytes 655360 | tf_op jit(solution)/shard_map/all_to_all | solution.py:141
  108.8 0.9 reduce_sum.38
  109.7 9.6 %all-to-all-done.3 = f32[32,4,640]{2,1,0:T(4,128)S(1)} async-done(((f32[32,4,640]{2,1,0:T(4,128)}), f32[32,4,640]{2,1,0:T(4,128)S(1)}, u32[]{:S(2)}, u32[]{:S(2)}) %all-to-all-start.3) | async-done | bytes 327712 | tf_op jit(solution)/shard_map/all_to_all | solution.py:141
  119.3 7.5 %all-to-all-start.8 = ((f32[32,8,512]{2,1,0:T(8,128)}), f32[32,8,512]{2,1,0:T(8,128)S(1)}, u32[]{:S(2)}, u32[]{:S(2)}) async-start(f32[32,8,512]{2,1,0:T(8,128)} %bitcast.9), calls=%async_computation.8 | async-start | bytes 1048576 | tf_op jit(solution)/shard_map/all_to_all | solution.py:141
  126.8 0.1 broadcast_in_dim.48
  126.9 14.1 %all-to-all-done.8 = f32[32,8,512]{2,1,0:T(8,128)S(1)} async-done(((f32[32,8,512]{2,1,0:T(8,128)}), f32[32,8,512]{2,1,0:T(8,128)S(1)}, u32[]{:S(2)}, u32[]{:S(2)}) %all-to-all-start.8) | async-done | bytes 524320 | tf_op jit(solution)/shard_map/all_to_all | solution.py:141
  141.0 0.9 broadcast_in_dim.49
  141.9 7.0 %all-to-all-start.4 = ((f32[2,128,640]{2,1,0:T(8,128)}), f32[2,128,640]{2,1,0:T(8,128)S(1)}, u32[]{:S(2)}, u32[]{:S(2)}) async-start(f32[2,128,640]{2,1,0:T(8,128)} %broadcast_in_dim.49), calls=%async_computation.4 | async-start | bytes 1310720 | tf_op jit(solution)/shard_map/all_to_all | solution.py:141
  148.9 1.4 all-to-all-done.4
  150.4 0.9 broadcast_in_dim.52
  151.2 5.4 %all-to-all-start.9 = ((f32[32,8,512]{2,1,0:T(8,128)}), f32[32,8,512]{2,1,0:T(8,128)S(1)}, u32[]{:S(2)}, u32[]{:S(2)}) async-start(f32[32,8,512]{2,1,0:T(8,128)} %broadcast_in_dim.52), calls=%async_computation.9 | async-start | bytes 1048576 | tf_op jit(solution)/shard_map/all_to_all | solution.py:141
  156.6 17.5 %shard_map.30 = f32[512,512]{1,0:T(8,128)S(1)} custom-call(f32[256,640]{1,0:T(8,128)S(1)} %bitcast.25), custom_call_target="tpu_custom_call" | custom-call | flops 2000000000 | bytes 2097152 | tf_op jit(solution)/shard_map/pallas_call | solution.py:128
  174.2 1.0 fusion
  175.2 1.0 copy.15
  176.2 0.0 all-to-all-done.9
  176.2 0.1 broadcast_in_dim.54
  176.3 4.9 %all_to_all.58 = f32[2,256,512]{2,1,0:T(8,128)S(1)} all-to-all(f32[2,256,512]{2,1,0:T(8,128)S(1)} %broadcast_in_dim.54), channel_id=1, replica_groups=mesh['x'=4,'y'=8,'core'=2,'col'=8] {'core'}, dimensions={0} | all-to-all | bytes 2097152 | tf_op jit(solution)/shard_map/all_to_all | solution.py:141
  181.2 2.8 %convolution_select_fusion = f32[512,512]{1,0:T(8,128)} fusion(f32[512,512]{1,0:T(8,128)S(1)} %shard_map.30, f32[512,512]{1,0:T(8,128)S(1)} %bitcast.28, pred[]{:T(512)S(6)} %eq.3), kind=kOutput, calls=%fused_computation | convolution fusion | flops 1611399168 | bytes 3145729 | tf_op jit(solution)/shard_map/dot_general | solution.py:31
  (5 shorter events, 0.1 us)
Async XLA Ops:
  32.1 23.1 %all-to-all-start.5 = ((f32[8,32,512]{2,1,0:T(8,128)}), f32[8,32,512]{2,1,0:T(8,128)S(1)}, u32[]{:S(2)}, u32[]{:S(2)}) async-start(f32[8,32,512]{2,1,0:T(8,128)} %bitcast.3), calls=%async_computation.5 | async-start | bytes 1048576 | tf_op jit(solution)/shard_map/all_to_all | solution.py:141
  55.8 10.7 %all-to-all-start.2 = ((f32[8,4,640]{2,1,0:T(4,128)}), f32[8,4,640]{2,1,0:T(4,128)S(1)}, u32[]{:S(2)}, u32[]{:S(2)}) async-start(f32[8,4,640]{2,1,0:T(4,128)} %broadcast_in_dim.45), calls=%async_computation.2 | async-start | bytes 163840 | tf_op jit(solution)/shard_map/all_to_all | solution.py:141
  67.4 15.7 %all-to-all-start.6 = ((f32[8,32,512]{2,1,0:T(8,128)}), f32[8,32,512]{2,1,0:T(8,128)S(1)}, u32[]{:S(2)}, u32[]{:S(2)}) async-start(f32[8,32,512]{2,1,0:T(8,128)} %broadcast_in_dim.51), calls=%async_computation.6 | async-start | bytes 1048576 | tf_op jit(solution)/shard_map/all_to_all | solution.py:141
  97.8 21.4 %all-to-all-start.3 = ((f32[32,4,640]{2,1,0:T(4,128)}), f32[32,4,640]{2,1,0:T(4,128)S(1)}, u32[]{:S(2)}, u32[]{:S(2)}) async-start(f32[32,4,640]{2,1,0:T(4,128)} %broadcast_in_dim.47), calls=%async_computation.3 | async-start | bytes 655360 | tf_op jit(solution)/shard_map/all_to_all | solution.py:141
  119.3 21.7 %all-to-all-start.8 = ((f32[32,8,512]{2,1,0:T(8,128)}), f32[32,8,512]{2,1,0:T(8,128)S(1)}, u32[]{:S(2)}, u32[]{:S(2)}) async-start(f32[32,8,512]{2,1,0:T(8,128)} %bitcast.9), calls=%async_computation.8 | async-start | bytes 1048576 | tf_op jit(solution)/shard_map/all_to_all | solution.py:141
  141.9 8.5 %all-to-all-start.4 = ((f32[2,128,640]{2,1,0:T(8,128)}), f32[2,128,640]{2,1,0:T(8,128)S(1)}, u32[]{:S(2)}, u32[]{:S(2)}) async-start(f32[2,128,640]{2,1,0:T(8,128)} %broadcast_in_dim.49), calls=%async_computation.4 | async-start | bytes 1310720 | tf_op jit(solution)/shard_map/all_to_all | solution.py:141
  151.2 25.0 %all-to-all-start.9 = ((f32[32,8,512]{2,1,0:T(8,128)}), f32[32,8,512]{2,1,0:T(8,128)S(1)}, u32[]{:S(2)}, u32[]{:S(2)}) async-start(f32[32,8,512]{2,1,0:T(8,128)} %broadcast_in_dim.52), calls=%async_computation.9 | async-start | bytes 1048576 | tf_op jit(solution)/shard_map/all_to_all | solution.py:141
